TPU v7x, 32 devices: a whole 2x2x4 slice. The times are simulated.
32 devices in a mesh: trial: 4 (over z), south: 2 (over core), east: 2 (over x), down: 2 (over y).
Axes of the slice: x: 2, y: 2, z: 4, core: 2. Of those that a mesh axis runs over, the one named last changes fastest.
Arguments:
- tracer: float32 [32, 32, 256, 128], P(('trial', 'south'), 'east', 'down'), parts along dimension 0, may hold values from 0.5 to 2
- mobility: float32 [32, 32, 256, 128], P(('trial', 'south'), 'east', 'down'), parts along dimension 0, may hold values from 0.03 to 0.15
- source: float32 [32, 32, 256, 128], P(('trial', 'south'), 'east', 'down'), parts along dimension 0, may hold values from -0.2 to 0.2
Outputs:
- standardized: float32 [32, 32, 256, 128], P(('trial', 'south'), 'east', 'down'), parts along dimension 0
- tracer_end: float32 [32, 32, 256, 128], P(('trial', 'south'), 'east', 'down'), parts along dimension 0
There are 4 independent parts, one for each index of `trial`. A program takes and returns all parts, laid end to end along the dimension named above; each array names one. Nothing has to cross between parts.
All inputs are finite; a program needn't handle non-finite values.
Results may differ from a plain program's by a relative error of at most 0.00002.
Values sent between devices are 32-bit elements; how exact they have to be, the bound alone decides.
A program may use at most 128 MiB of HBM per device.

v0:
```python
import jax
import jax.numpy as jnp
from jax import lax
from jax.sharding import PartitionSpec as P

STEPS = 3


def with_halo(block, sides, width):
    for axis, dim in sides:
        count = lax.axis_size(axis)
        forward = [(i, i + 1) for i in range(count - 1)]
        forward.append((count - 1, 0))
        backward = [(target, source) for source, target in forward]
        low = lax.ppermute(
            lax.slice_in_dim(block, block.shape[dim] - width, None, axis=dim), axis, forward
        )
        high = lax.ppermute(lax.slice_in_dim(block, 0, width, axis=dim), axis, backward)
        block = jnp.concatenate([low, block, high], axis=dim)
    return block


def strip_edges(values, dims):
    for dim in dims:
        values = lax.slice_in_dim(values, 1, values.shape[dim] - 1, axis=dim)
    return values


def neighbour(values, dim, start, dims):
    others = [other for other in dims if other != dim]
    values = strip_edges(values, others)
    return lax.slice_in_dim(values, start, start + values.shape[dim] - 2, axis=dim)


def one_step(padded, mobility, source):
    middle = strip_edges(padded, (0, 1, 2))
    lower = [neighbour(padded, dim, 0, (0, 1, 2)) for dim in (0, 1, 2)]
    upper = [neighbour(padded, dim, 2, (0, 1, 2)) for dim in (0, 1, 2)]
    spread = lower[0] + upper[0] + lower[1] + upper[1] + lower[2] + upper[2] - 6.0 * middle
    return middle + mobility * spread + source


def body(tracer, mobility, source):
    for step in range(STEPS):
        padded = with_halo(tracer, (("south", 0), ("east", 1), ("down", 2)), 1)
        tracer = one_step(padded, mobility, source)
    count = tracer.shape[2] * lax.axis_size("down")
    line_mean = lax.psum(jnp.sum(tracer, axis=2, keepdims=True), "down") / count
    centred = tracer - line_mean
    line_variance = lax.psum(jnp.sum(centred * centred, axis=2, keepdims=True), "down") / count
    standardized = centred * lax.rsqrt(line_variance + 0.0001)
    return (standardized, tracer)


def solution(mesh):
    in_specs = (
        P(("trial", "south"), "east", "down", None),
        P(("trial", "south"), "east", "down", None),
        P(("trial", "south"), "east", "down", None),
    )
    out_specs = (
        P(("trial", "south"), "east", "down", None),
        P(("trial", "south"), "east", "down", None),
    )
    return jax.shard_map(body, mesh=mesh, in_specs=in_specs, out_specs=out_specs, check_vma=False)
```

profile of v0, /device:TPU:0, one launch (start us, length us, event | category | flops | bytes accessed | tf_op | source)
XLA Modules:
  0.0 147.4 jit_solution(11715911265367690488)
XLA Ops:
  0.6 1.8 %fusion.32 = (f32[1,16,128,128]{3,2,1,0:T(8,128)S(1)}, f32[1,16,128,128]{3,2,1,0:T(8,128)S(1)}) fusion(f32[4,16,128,128]{3,2,1,0:T(8,128)} %param.3), kind=kLoop, calls=%fused_computation.103 | loop fusion | bytes 4194304 | tf_op jit(solution)/shard_map/slice | solution.py:18
  2.5 0.6 collective-permute-start
  3.0 0.1 collective-permute-start.1
  3.1 2.2 %collective-permute-done = f32[1,16,128,128]{3,2,1,0:T(8,128)S(1)} collective-permute-done((f32[1,16,128,128]{3,2,1,0:T(8,128)S(1)}, f32[1,16,128,128]{3,2,1,0:T(8,128)S(1)}, u32[]{:S(2)}, u32[]{:S(2)}) %collective-permute-start) | collective-permute-done | bytes 1048608 | tf_op jit(solution)/shard_map/ppermute | solution.py:15
  5.3 0.1 constant_dynamic-update-slice_fusion.2
  5.4 0.5 constant_dynamic-update-slice_fusion.1
  5.9 0.9 collective-permute-done.1
  6.8 0.1 constant_dynamic-update-slice_fusion
  7.0 2.9 %collective-permute-start.2 = (f32[6,1,128,128]{3,2,1,0:T(8,128)S(1)}, f32[6,1,128,128]{3,2,1,0:T(8,128)S(1)}, u32[]{:S(2)}, u32[]{:S(2)}) collective-permute-start(f32[6,1,128,128]{3,2,1,0:T(8,128)S(1)} %get-tuple-element.14), channel_id=1, source_target_pairs={{0,2},{2,0},{1,3},{3,1},{4,6},{6,4},{5,7},{7,5},{8,10},{10,8},{9,1... | collective-permute-start | bytes 1179656 | tf_op jit(solution)/shard_map/ppermute | solution.py:15
  9.9 0.1 collective-permute-start.3
  10.0 9.9 %collective-permute-done.2 = f32[6,1,128,128]{3,2,1,0:T(8,128)S(1)} collective-permute-done((f32[6,1,128,128]{3,2,1,0:T(8,128)S(1)}, f32[6,1,128,128]{3,2,1,0:T(8,128)S(1)}, u32[]{:S(2)}, u32[]{:S(2)}) %collective-permute-start.2) | collective-permute-done | bytes 393248 | tf_op jit(solution)/shard_map/ppermute | solution.py:15
  19.9 7.9 %collective-permute-done.3 = f32[6,1,128,128]{3,2,1,0:T(8,128)S(1)} collective-permute-done((f32[6,1,128,128]{3,2,1,0:T(8,128)S(1)}, f32[6,1,128,128]{3,2,1,0:T(8,128)S(1)}, u32[]{:S(2)}, u32[]{:S(2)}) %collective-permute-start.3) | collective-permute-done | bytes 393248 | tf_op jit(solution)/shard_map/ppermute | solution.py:18
  27.8 0.1 pad_maximum_fusion.64
  27.9 1.8 %collective-permute-start.4 = (f32[6,18,1,128]{3,2,1,0:T(1,128)S(1)}, f32[6,18,1,128]{3,2,1,0:T(1,128)S(1)}, u32[]{:S(2)}, u32[]{:S(2)}) collective-permute-start(f32[6,18,1,128]{3,2,1,0:T(1,128)S(1)} %get-tuple-element.8), channel_id=1, source_target_pairs={{0,1},{1,0},{2,3},{3,2},{4,5},{5,4},{6,7},{7,6},{8,9},{9,8},{10,11... | collective-permute-start | bytes 165896 | tf_op jit(solution)/shard_map/ppermute | solution.py:15
  29.7 0.3 collective-permute-start.5
  29.9 2.5 %collective-permute-done.4 = f32[6,18,1,128]{3,2,1,0:T(1,128)S(1)} collective-permute-done((f32[6,18,1,128]{3,2,1,0:T(1,128)S(1)}, f32[6,18,1,128]{3,2,1,0:T(1,128)S(1)}, u32[]{:S(2)}, u32[]{:S(2)}) %collective-permute-start.4) | collective-permute-done | bytes 55328 | tf_op jit(solution)/shard_map/ppermute | solution.py:15
  32.5 1.4 collective-permute-done.5
  33.8 13.8 %fusion.22 = f32[4,16,128,128]{3,2,1,0:T(8,128)S(1)} fusion(f32[4,16,128,128]{3,2,1,0:T(8,128)S(1)} %copy-done, f32[4,16,128,128]{3,2,1,0:T(8,128)} %param.3, f32[4,16,128,128]{3,2,1,0:T(8,128)} %param.4, f32[6,18,1,128]{3,2,1,0:T(1,128)S(1)} %collective-permute-done.5, f32[6,1,128,128]{3,2,1,0:T(8,128)S(1)} %collective-permute-done.3, ...), kind=kLoop, calls=%fused_computation.59 | loop fusion | flops 20971520 | bytes 26062848 | tf_op jit(solution)/shard_map/add | solution.py:40
  47.6 0.1 fusion.31
  47.8 0.5 collective-permute-start.7
  48.3 2.1 %collective-permute-done.6 = f32[1,16,128,128]{3,2,1,0:T(8,128)S(1)} collective-permute-done((f32[1,16,128,128]{3,2,1,0:T(8,128)S(1)}, f32[1,16,128,128]{3,2,1,0:T(8,128)S(1)}, u32[]{:S(2)}, u32[]{:S(2)}) %collective-permute-start.6) | collective-permute-done | bytes 1048608 | tf_op jit(solution)/shard_map/ppermute | solution.py:15
  50.5 1.5 %collective-permute-done.7 = f32[1,16,128,128]{3,2,1,0:T(8,128)S(1)} collective-permute-done((f32[1,16,128,128]{3,2,1,0:T(8,128)S(1)}, f32[1,16,128,128]{3,2,1,0:T(8,128)S(1)}, u32[]{:S(2)}, u32[]{:S(2)}) %collective-permute-start.7) | collective-permute-done | bytes 1048608 | tf_op jit(solution)/shard_map/ppermute | solution.py:18
  52.1 1.6 %collective-permute-start.8 = (f32[6,1,128,128]{3,2,1,0:T(8,128)S(1)}, f32[6,1,128,128]{3,2,1,0:T(8,128)S(1)}, u32[]{:S(2)}, u32[]{:S(2)}) collective-permute-start(f32[6,1,128,128]{3,2,1,0:T(8,128)S(1)} %get-tuple-element.12), channel_id=1, source_target_pairs={{0,2},{2,0},{1,3},{3,1},{4,6},{6,4},{5,7},{7,5},{8,10},{10,8},{9,1... | collective-permute-start | bytes 1179656 | tf_op jit(solution)/shard_map/ppermute | solution.py:15
  53.6 0.5 collective-permute-start.9
  54.2 10.0 %collective-permute-done.8 = f32[6,1,128,128]{3,2,1,0:T(8,128)S(1)} collective-permute-done((f32[6,1,128,128]{3,2,1,0:T(8,128)S(1)}, f32[6,1,128,128]{3,2,1,0:T(8,128)S(1)}, u32[]{:S(2)}, u32[]{:S(2)}) %collective-permute-start.8) | collective-permute-done | bytes 393248 | tf_op jit(solution)/shard_map/ppermute | solution.py:15
  64.1 7.6 %collective-permute-done.9 = f32[6,1,128,128]{3,2,1,0:T(8,128)S(1)} collective-permute-done((f32[6,1,128,128]{3,2,1,0:T(8,128)S(1)}, f32[6,1,128,128]{3,2,1,0:T(8,128)S(1)}, u32[]{:S(2)}, u32[]{:S(2)}) %collective-permute-start.9) | collective-permute-done | bytes 393248 | tf_op jit(solution)/shard_map/ppermute | solution.py:18
  71.8 0.7 collective-permute-start.10
  72.5 1.4 collective-permute-start.11
  73.9 2.1 %collective-permute-done.10 = f32[6,18,1,128]{3,2,1,0:T(1,128)S(1)} collective-permute-done((f32[6,18,1,128]{3,2,1,0:T(1,128)S(1)}, f32[6,18,1,128]{3,2,1,0:T(1,128)S(1)}, u32[]{:S(2)}, u32[]{:S(2)}) %collective-permute-start.10) | collective-permute-done | bytes 55328 | tf_op jit(solution)/shard_map/ppermute | solution.py:15
  76.0 0.6 collective-permute-done.11
  76.6 7.6 %fusion.13 = f32[4,16,128,128]{3,2,1,0:T(8,128)S(1)} fusion(f32[4,16,128,128]{3,2,1,0:T(8,128)S(1)} %copy-done, f32[4,16,128,128]{3,2,1,0:T(8,128)S(1)} %fusion.22, f32[4,16,128,128]{3,2,1,0:T(8,128)S(1)} %copy-done.1, f32[6,18,1,128]{3,2,1,0:T(1,128)S(1)} %collective-permute-done.11, f32[6,1,128,128]{3,2,1,0:T(8,128)S(1)} %collective-permute-done.9, ...), kind=kLoop, calls=%fused_computation.32 | loop fusion | flops 29360128 | bytes 19771392 | tf_op jit(solution)/shard_map/add | solution.py:40
  84.2 0.2 fusion.30
  84.5 0.5 collective-permute-start.13
  85.0 2.1 %collective-permute-done.12 = f32[1,16,128,128]{3,2,1,0:T(8,128)S(1)} collective-permute-done((f32[1,16,128,128]{3,2,1,0:T(8,128)S(1)}, f32[1,16,128,128]{3,2,1,0:T(8,128)S(1)}, u32[]{:S(2)}, u32[]{:S(2)}) %collective-permute-start.12) | collective-permute-done | bytes 1048608 | tf_op jit(solution)/shard_map/ppermute | solution.py:15
  87.2 1.5 %collective-permute-done.13 = f32[1,16,128,128]{3,2,1,0:T(8,128)S(1)} collective-permute-done((f32[1,16,128,128]{3,2,1,0:T(8,128)S(1)}, f32[1,16,128,128]{3,2,1,0:T(8,128)S(1)}, u32[]{:S(2)}, u32[]{:S(2)}) %collective-permute-start.13) | collective-permute-done | bytes 1048608 | tf_op jit(solution)/shard_map/ppermute | solution.py:18
  88.7 1.6 %collective-permute-start.14 = (f32[6,1,128,128]{3,2,1,0:T(8,128)S(1)}, f32[6,1,128,128]{3,2,1,0:T(8,128)S(1)}, u32[]{:S(2)}, u32[]{:S(2)}) collective-permute-start(f32[6,1,128,128]{3,2,1,0:T(8,128)S(1)} %get-tuple-element.10), channel_id=1, source_target_pairs={{0,2},{2,0},{1,3},{3,1},{4,6},{6,4},{5,7},{7,5},{8,10},{10,8},{9,1... | collective-permute-start | bytes 1179656 | tf_op jit(solution)/shard_map/ppermute | solution.py:15
  90.3 0.5 collective-permute-start.15
  90.8 10.0 %collective-permute-done.14 = f32[6,1,128,128]{3,2,1,0:T(8,128)S(1)} collective-permute-done((f32[6,1,128,128]{3,2,1,0:T(8,128)S(1)}, f32[6,1,128,128]{3,2,1,0:T(8,128)S(1)}, u32[]{:S(2)}, u32[]{:S(2)}) %collective-permute-start.14) | collective-permute-done | bytes 393248 | tf_op jit(solution)/shard_map/ppermute | solution.py:15
  100.8 7.6 %collective-permute-done.15 = f32[6,1,128,128]{3,2,1,0:T(8,128)S(1)} collective-permute-done((f32[6,1,128,128]{3,2,1,0:T(8,128)S(1)}, f32[6,1,128,128]{3,2,1,0:T(8,128)S(1)}, u32[]{:S(2)}, u32[]{:S(2)}) %collective-permute-start.15) | collective-permute-done | bytes 393248 | tf_op jit(solution)/shard_map/ppermute | solution.py:18
  108.4 1.5 %collective-permute-start.16 = (f32[6,18,1,128]{3,2,1,0:T(1,128)S(1)}, f32[6,18,1,128]{3,2,1,0:T(1,128)S(1)}, u32[]{:S(2)}, u32[]{:S(2)}) collective-permute-start(f32[6,18,1,128]{3,2,1,0:T(1,128)S(1)} %get-tuple-element.4), channel_id=1, source_target_pairs={{0,1},{1,0},{2,3},{3,2},{4,5},{5,4},{6,7},{7,6},{8,9},{9,8},{10,11... | collective-permute-start | bytes 165896 | tf_op jit(solution)/shard_map/ppermute | solution.py:15
  109.9 0.6 collective-permute-start.17
  110.5 2.2 %collective-permute-done.16 = f32[6,18,1,128]{3,2,1,0:T(1,128)S(1)} collective-permute-done((f32[6,18,1,128]{3,2,1,0:T(1,128)S(1)}, f32[6,18,1,128]{3,2,1,0:T(1,128)S(1)}, u32[]{:S(2)}, u32[]{:S(2)}) %collective-permute-start.16) | collective-permute-done | bytes 55328 | tf_op jit(solution)/shard_map/ppermute | solution.py:15
  112.7 1.4 collective-permute-done.17
  114.1 9.3 %fusion.27 = (f32[4,16,128]{2,1,0:T(8,128)S(1)}, f32[4,16,128,128]{3,2,1,0:T(8,128)}) fusion(f32[4,16,128,128]{3,2,1,0:T(8,128)S(1)} %copy-done, f32[4,16,128,128]{3,2,1,0:T(8,128)S(1)} %fusion.13, f32[4,16,128,128]{3,2,1,0:T(8,128)S(1)} %copy-done.1, f32[6,18,1,128]{3,2,1,0:T(1,128)S(1)} %collective-permute-done.17, ...), kind=kLoop, calls=%fused_computation.99 | loop fusion | flops 30400512 | bytes 19804160 | tf_op jit(solution)/shard_map/reduce_sum | solution.py:48
  123.4 7.4 %psum.14 = f32[4,16,1,128]{3,1,0,2:T(8,128)S(1)} all-reduce(f32[4,16,1,128]{3,1,0,2:T(8,128)S(1)} %bitcast.6), channel_id=1, replica_groups=mesh['trial'=4,'south'=2,'east'=2,'down'=2] {'down'}, use_global_device_ids=true, to_apply=%region_1.0 | all-reduce | flops 8192 | bytes 65536 | tf_op jit(solution)/shard_map/psum | solution.py:48
  130.8 3.0 %multiply_reduce_fusion = f32[4,16,128]{2,1,0:T(8,128)S(1)} fusion(f32[4,16,128,128]{3,2,1,0:T(8,128)} %get-tuple-element.3, f32[4,16,128]{2,1,0:T(8,128)S(1)} %multiply_bitcast_fusion), kind=kLoop, calls=%fused_computation.73 | loop fusion | flops 3137536 | bytes 4259840 | tf_op jit(solution)/shard_map/reduce_sum | solution.py:50
  133.8 8.3 %psum.15 = f32[4,16,1,128]{3,1,0,2:T(8,128)S(1)} all-reduce(f32[4,16,1,128]{3,1,0,2:T(8,128)S(1)} %bitcast.7), channel_id=1, replica_groups=mesh['trial'=4,'south'=2,'east'=2,'down'=2] {'down'}, use_global_device_ids=true, to_apply=%region_3.0 | all-reduce | flops 8192 | bytes 65536 | tf_op jit(solution)/shard_map/psum | solution.py:50
  142.1 5.2 %subtract_multiply_fusion = f32[4,16,128,128]{3,2,1,0:T(8,128)} fusion(f32[4,16,128,128]{3,2,1,0:T(8,128)} %get-tuple-element.3, f32[4,16,128]{2,1,0:T(8,128)S(1)} %rsqrt_bitcast_fusion, f32[4,16,128]{2,1,0:T(8,128)S(1)} %multiply_bitcast_fusion), kind=kLoop, calls=%fused_computation.74 | loop fusion | flops 2097152 | bytes 8454144 | tf_op jit(solution)/shard_map/mul | solution.py:51
  (17 shorter events, 0.5 us)
Async XLA Ops:
  0.6 4.8 %copy-start.3 = (f32[4,16,128,128]{3,2,1,0:T(8,128)S(1)}, f32[4,16,128,128]{3,2,1,0:T(8,128)}, u32[]{:S(2)}) copy-start(f32[4,16,128,128]{3,2,1,0:T(8,128)} %param.3) | copy-start | bytes 12582916
  2.5 2.8 %collective-permute-start = (f32[1,16,128,128]{3,2,1,0:T(8,128)S(1)}, f32[1,16,128,128]{3,2,1,0:T(8,128)S(1)}, u32[]{:S(2)}, u32[]{:S(2)}) collective-permute-start(f32[1,16,128,128]{3,2,1,0:T(8,128)S(1)} %get-tuple-element.21), channel_id=1, source_target_pairs={{0,4},{4,0},{1,5},{5,1},{2,6},{6,2},{3,7},{7,3},{8,12},{12,8},{9,1... | collective-permute-start | bytes 3145736 | tf_op jit(solution)/shard_map/ppermute | solution.py:15
  3.0 3.8 %collective-permute-start.1 = (f32[1,16,128,128]{3,2,1,0:T(8,128)S(1)}, f32[1,16,128,128]{3,2,1,0:T(8,128)S(1)}, u32[]{:S(2)}, u32[]{:S(2)}) collective-permute-start(f32[1,16,128,128]{3,2,1,0:T(8,128)S(1)} %get-tuple-element.20), channel_id=1, source_target_pairs={{4,0},{0,4},{5,1},{1,5},{6,2},{2,6},{7,3},{3,7},{12,8},{8,12},{13,... | collective-permute-start | bytes 3145736 | tf_op jit(solution)/shard_map/ppermute | solution.py:18
  6.9 25.5 %copy-start.2 = (f32[6,16,128,128]{3,2,1,0:T(8,128)}, f32[6,16,128,128]{3,2,1,0:T(8,128)S(1)}, u32[]{:S(2)}) copy-start(f32[6,16,128,128]{3,2,1,0:T(8,128)S(1)} %constant_dynamic-update-slice_fusion) | copy-start | bytes 18874372
  6.9 26.9 %copy-start = (f32[4,16,128,128]{3,2,1,0:T(8,128)S(1)}, f32[4,16,128,128]{3,2,1,0:T(8,128)}, u32[]{:S(2)}) copy-start(f32[4,16,128,128]{3,2,1,0:T(8,128)} %param.5) | copy-start | bytes 12582916
  7.0 12.9 %collective-permute-start.2 = (f32[6,1,128,128]{3,2,1,0:T(8,128)S(1)}, f32[6,1,128,128]{3,2,1,0:T(8,128)S(1)}, u32[]{:S(2)}, u32[]{:S(2)}) collective-permute-start(f32[6,1,128,128]{3,2,1,0:T(8,128)S(1)} %get-tuple-element.14), channel_id=1, source_target_pairs={{0,2},{2,0},{1,3},{3,1},{4,6},{6,4},{5,7},{7,5},{8,10},{10,8},{9,1... | collective-permute-start | bytes 1179656 | tf_op jit(solution)/shard_map/ppermute | solution.py:15
  9.9 17.8 %collective-permute-start.3 = (f32[6,1,128,128]{3,2,1,0:T(8,128)S(1)}, f32[6,1,128,128]{3,2,1,0:T(8,128)S(1)}, u32[]{:S(2)}, u32[]{:S(2)}) collective-permute-start(f32[6,1,128,128]{3,2,1,0:T(8,128)S(1)} %get-tuple-element.15), channel_id=1, source_target_pairs={{2,0},{0,2},{3,1},{1,3},{6,4},{4,6},{7,5},{5,7},{10,8},{8,10},{11,... | collective-permute-start | bytes 1179656 | tf_op jit(solution)/shard_map/ppermute | solution.py:18
  27.9 4.6 %collective-permute-start.4 = (f32[6,18,1,128]{3,2,1,0:T(1,128)S(1)}, f32[6,18,1,128]{3,2,1,0:T(1,128)S(1)}, u32[]{:S(2)}, u32[]{:S(2)}) collective-permute-start(f32[6,18,1,128]{3,2,1,0:T(1,128)S(1)} %get-tuple-element.8), channel_id=1, source_target_pairs={{0,1},{1,0},{2,3},{3,2},{4,5},{5,4},{6,7},{7,6},{8,9},{9,8},{10,11... | collective-permute-start | bytes 165896 | tf_op jit(solution)/shard_map/ppermute | solution.py:15
  29.7 4.2 %collective-permute-start.5 = (f32[6,18,1,128]{3,2,1,0:T(1,128)S(1)}, f32[6,18,1,128]{3,2,1,0:T(1,128)S(1)}, u32[]{:S(2)}, u32[]{:S(2)}) collective-permute-start(f32[6,18,1,128]{3,2,1,0:T(1,128)S(1)} %get-tuple-element.9), channel_id=1, source_target_pairs={{1,0},{0,1},{3,2},{2,3},{5,4},{4,5},{7,6},{6,7},{9,8},{8,9},{11,10... | collective-permute-start | bytes 165896 | tf_op jit(solution)/shard_map/ppermute | solution.py:18
  47.8 2.7 %collective-permute-start.6 = (f32[1,16,128,128]{3,2,1,0:T(8,128)S(1)}, f32[1,16,128,128]{3,2,1,0:T(8,128)S(1)}, u32[]{:S(2)}, u32[]{:S(2)}) collective-permute-start(f32[1,16,128,128]{3,2,1,0:T(8,128)S(1)} %get-tuple-element.18), channel_id=1, source_target_pairs={{0,4},{4,0},{1,5},{5,1},{2,6},{6,2},{3,7},{7,3},{8,12},{12,8},{9,1... | collective-permute-start | bytes 3145736 | tf_op jit(solution)/shard_map/ppermute | solution.py:15
  47.8 4.1 %collective-permute-start.7 = (f32[1,16,128,128]{3,2,1,0:T(8,128)S(1)}, f32[1,16,128,128]{3,2,1,0:T(8,128)S(1)}, u32[]{:S(2)}, u32[]{:S(2)}) collective-permute-start(f32[1,16,128,128]{3,2,1,0:T(8,128)S(1)} %get-tuple-element.19), channel_id=1, source_target_pairs={{4,0},{0,4},{5,1},{1,5},{6,2},{2,6},{7,3},{3,7},{12,8},{8,12},{13,... | collective-permute-start | bytes 3145736 | tf_op jit(solution)/shard_map/ppermute | solution.py:18
  52.1 24.6 %copy-start.1 = (f32[4,16,128,128]{3,2,1,0:T(8,128)S(1)}, f32[4,16,128,128]{3,2,1,0:T(8,128)}, u32[]{:S(2)}) copy-start(f32[4,16,128,128]{3,2,1,0:T(8,128)} %param.4) | copy-start | bytes 12582916
  52.1 12.1 %collective-permute-start.8 = (f32[6,1,128,128]{3,2,1,0:T(8,128)S(1)}, f32[6,1,128,128]{3,2,1,0:T(8,128)S(1)}, u32[]{:S(2)}, u32[]{:S(2)}) collective-permute-start(f32[6,1,128,128]{3,2,1,0:T(8,128)S(1)} %get-tuple-element.12), channel_id=1, source_target_pairs={{0,2},{2,0},{1,3},{3,1},{4,6},{6,4},{5,7},{7,5},{8,10},{10,8},{9,1... | collective-permute-start | bytes 1179656 | tf_op jit(solution)/shard_map/ppermute | solution.py:15
  53.6 18.1 %collective-permute-start.9 = (f32[6,1,128,128]{3,2,1,0:T(8,128)S(1)}, f32[6,1,128,128]{3,2,1,0:T(8,128)S(1)}, u32[]{:S(2)}, u32[]{:S(2)}) collective-permute-start(f32[6,1,128,128]{3,2,1,0:T(8,128)S(1)} %get-tuple-element.13), channel_id=1, source_target_pairs={{2,0},{0,2},{3,1},{1,3},{6,4},{4,6},{7,5},{5,7},{10,8},{8,10},{11,... | collective-permute-start | bytes 1179656 | tf_op jit(solution)/shard_map/ppermute | solution.py:18
  71.8 4.2 %collective-permute-start.10 = (f32[6,18,1,128]{3,2,1,0:T(1,128)S(1)}, f32[6,18,1,128]{3,2,1,0:T(1,128)S(1)}, u32[]{:S(2)}, u32[]{:S(2)}) collective-permute-start(f32[6,18,1,128]{3,2,1,0:T(1,128)S(1)} %get-tuple-element.6), channel_id=1, source_target_pairs={{0,1},{1,0},{2,3},{3,2},{4,5},{5,4},{6,7},{7,6},{8,9},{9,8},{10,11... | collective-permute-start | bytes 165896 | tf_op jit(solution)/shard_map/ppermute | solution.py:15
  72.5 4.2 %collective-permute-start.11 = (f32[6,18,1,128]{3,2,1,0:T(1,128)S(1)}, f32[6,18,1,128]{3,2,1,0:T(1,128)S(1)}, u32[]{:S(2)}, u32[]{:S(2)}) collective-permute-start(f32[6,18,1,128]{3,2,1,0:T(1,128)S(1)} %get-tuple-element.7), channel_id=1, source_target_pairs={{1,0},{0,1},{3,2},{2,3},{5,4},{4,5},{7,6},{6,7},{9,8},{8,9},{11,10... | collective-permute-start | bytes 165896 | tf_op jit(solution)/shard_map/ppermute | solution.py:18
  84.4 2.7 %collective-permute-start.12 = (f32[1,16,128,128]{3,2,1,0:T(8,128)S(1)}, f32[1,16,128,128]{3,2,1,0:T(8,128)S(1)}, u32[]{:S(2)}, u32[]{:S(2)}) collective-permute-start(f32[1,16,128,128]{3,2,1,0:T(8,128)S(1)} %get-tuple-element.16), channel_id=1, source_target_pairs={{0,4},{4,0},{1,5},{5,1},{2,6},{6,2},{3,7},{7,3},{8,12},{12,8},{9,1... | collective-permute-start | bytes 3145736 | tf_op jit(solution)/shard_map/ppermute | solution.py:15
  84.5 4.1 %collective-permute-start.13 = (f32[1,16,128,128]{3,2,1,0:T(8,128)S(1)}, f32[1,16,128,128]{3,2,1,0:T(8,128)S(1)}, u32[]{:S(2)}, u32[]{:S(2)}) collective-permute-start(f32[1,16,128,128]{3,2,1,0:T(8,128)S(1)} %get-tuple-element.17), channel_id=1, source_target_pairs={{4,0},{0,4},{5,1},{1,5},{6,2},{2,6},{7,3},{3,7},{12,8},{8,12},{13,... | collective-permute-start | bytes 3145736 | tf_op jit(solution)/shard_map/ppermute | solution.py:18
  88.7 12.1 %collective-permute-start.14 = (f32[6,1,128,128]{3,2,1,0:T(8,128)S(1)}, f32[6,1,128,128]{3,2,1,0:T(8,128)S(1)}, u32[]{:S(2)}, u32[]{:S(2)}) collective-permute-start(f32[6,1,128,128]{3,2,1,0:T(8,128)S(1)} %get-tuple-element.10), channel_id=1, source_target_pairs={{0,2},{2,0},{1,3},{3,1},{4,6},{6,4},{5,7},{7,5},{8,10},{10,8},{9,1... | collective-permute-start | bytes 1179656 | tf_op jit(solution)/shard_map/ppermute | solution.py:15
  90.3 18.1 %collective-permute-start.15 = (f32[6,1,128,128]{3,2,1,0:T(8,128)S(1)}, f32[6,1,128,128]{3,2,1,0:T(8,128)S(1)}, u32[]{:S(2)}, u32[]{:S(2)}) collective-permute-start(f32[6,1,128,128]{3,2,1,0:T(8,128)S(1)} %get-tuple-element.11), channel_id=1, source_target_pairs={{2,0},{0,2},{3,1},{1,3},{6,4},{4,6},{7,5},{5,7},{10,8},{8,10},{11,... | collective-permute-start | bytes 1179656 | tf_op jit(solution)/shard_map/ppermute | solution.py:18
  108.4 4.3 %collective-permute-start.16 = (f32[6,18,1,128]{3,2,1,0:T(1,128)S(1)}, f32[6,18,1,128]{3,2,1,0:T(1,128)S(1)}, u32[]{:S(2)}, u32[]{:S(2)}) collective-permute-start(f32[6,18,1,128]{3,2,1,0:T(1,128)S(1)} %get-tuple-element.4), channel_id=1, source_target_pairs={{0,1},{1,0},{2,3},{3,2},{4,5},{5,4},{6,7},{7,6},{8,9},{9,8},{10,11... | collective-permute-start | bytes 165896 | tf_op jit(solution)/shard_map/ppermute | solution.py:15
  109.9 4.2 %collective-permute-start.17 = (f32[6,18,1,128]{3,2,1,0:T(1,128)S(1)}, f32[6,18,1,128]{3,2,1,0:T(1,128)S(1)}, u32[]{:S(2)}, u32[]{:S(2)}) collective-permute-start(f32[6,18,1,128]{3,2,1,0:T(1,128)S(1)} %get-tuple-element.5), channel_id=1, source_target_pairs={{1,0},{0,1},{3,2},{2,3},{5,4},{4,5},{7,6},{6,7},{9,8},{8,9},{11,10... | collective-permute-start | bytes 165896 | tf_op jit(solution)/shard_map/ppermute | solution.py:18
where the time goes:
time: 148 us; the launch traced here: 147 us
  waiting for transfers between devices  73.5 us (50%)
  other arithmetic  39.2 us (26%)
  blocking collectives  15.7 us (11%)
  starting transfers between devices  15.2 us (10%)
  local copies, waits for them, and re-layouts  2.94 us (2%)
    ppermute x9, waiting for transfers between devices, with_halo(): lax.ppermute(lax.slice_in_dim(block, block.shape[dim] - width, None, axis...  43.1 us
    ppermute x9, waiting for transfers between devices, with_halo(): lax.ppermute(lax.slice_in_dim(block, 0, width, axis=dim), axis, backward)  30.3 us
    add x2, other arithmetic, one_step(): return middle + mobility * spread + source  21.3 us
    ppermute x9, starting transfers between devices, with_halo(): lax.ppermute(lax.slice_in_dim(block, block.shape[dim] - width, None, axis...  10.7 us
    reduce_sum x1, other arithmetic, body(): line_mean = lax.psum(jnp.sum(tracer, axis=2, keepdims=True), 'down') / count  9.27 us
    psum x1, blocking collectives, body(): lax.psum(jnp.sum(centred * centred, axis=2, keepdims=True), 'down') / count  8.28 us
    psum x1, blocking collectives, body(): line_mean = lax.psum(jnp.sum(tracer, axis=2, keepdims=True), 'down') / count  7.43 us
    mul x2, other arithmetic, body(): standardized = centred * lax.rsqrt(line_variance + 0.0001)  5.24 us
  transfers between devices with their start and end apart: 18, of which 18 were waited for; matrix products, arithmetic and copies ran while one was open for 0% of the time, Pallas kernels for 0%

commit v1 on v0

--- a/solution.py
+++ b/solution.py
@@ -47,7 +47,10 @@
     count = tracer.shape[2] * lax.axis_size("down")
     line_mean = lax.psum(jnp.sum(tracer, axis=2, keepdims=True), "down") / count
     centred = tracer - line_mean
-    line_variance = lax.psum(jnp.sum(centred * centred, axis=2, keepdims=True), "down") / count
+    line_variance = (
+        jnp.sum(lax.all_gather(jnp.sum(centred * centred, axis=2, keepdims=True), "down"), axis=0)
+        / count
+    )
     standardized = centred * lax.rsqrt(line_variance + 0.0001)
     return (standardized, tracer)
 

time: 148 us -> 144 us (0.973)
  blocking collectives: 15.7 us -> 12 us
    psum x1 -> x0, blocking collectives: 8.28 us -> none  [body(): lax.psum(jnp.sum(centred * centred, axis=2, keepdims=True), 'down') / count]
    all_gather x0 -> x1, blocking collectives: none -> 4.58 us  [body(): lax.all_gather(jnp.sum(centred * centred, axis=2, keepdims=True), 'down')]
    mul x2 -> x1, other arithmetic: 5.24 us -> 5.23 us  [body(): standardized = centred * lax.rsqrt(line_variance + 0.0001)]
where the time goes in v1:
time: 144 us
  waiting for transfers between devices  73.5 us (51%)
  other arithmetic  39.2 us (27%)
  starting transfers between devices  15.2 us (11%)
  blocking collectives  12 us (8%)
  local copies, waits for them, and re-layouts  2.94 us (2%)
    ppermute x9, waiting for transfers between devices, with_halo(): lax.ppermute(lax.slice_in_dim(block, block.shape[dim] - width, None, axis...  43.1 us
    ppermute x9, waiting for transfers between devices, with_halo(): lax.ppermute(lax.slice_in_dim(block, 0, width, axis=dim), axis, backward)  30.3 us
    add x2, other arithmetic, one_step(): return middle + mobility * spread + source  21.3 us
    ppermute x9, starting transfers between devices, with_halo(): lax.ppermute(lax.slice_in_dim(block, block.shape[dim] - width, None, axis...  10.7 us
    reduce_sum x1, other arithmetic, body(): line_mean = lax.psum(jnp.sum(tracer, axis=2, keepdims=True), 'down') / count  9.27 us
    psum x1, blocking collectives, body(): line_mean = lax.psum(jnp.sum(tracer, axis=2, keepdims=True), 'down') / count  7.43 us
    mul x1, other arithmetic, body(): standardized = centred * lax.rsqrt(line_variance + 0.0001)  5.23 us
    all_gather x1, blocking collectives, body(): lax.all_gather(jnp.sum(centred * centred, axis=2, keepdims=True), 'down')  4.58 us
  transfers between devices with their start and end apart: 18, of which 18 were waited for; matrix products, arithmetic and copies ran while one was open for 0% of the time, Pallas kernels for 0%

profile of v1, /device:TPU:0, one launch (start us, length us, event | category | flops | bytes accessed | tf_op | source)
XLA Modules:
  0.0 143.6 jit_solution(6873449629453028008)
XLA Ops:
  0.6 1.8 %fusion.32 = (f32[1,16,128,128]{3,2,1,0:T(8,128)S(1)}, f32[1,16,128,128]{3,2,1,0:T(8,128)S(1)}) fusion(f32[4,16,128,128]{3,2,1,0:T(8,128)} %param.3), kind=kLoop, calls=%fused_computation.103 | loop fusion | bytes 4194304 | tf_op jit(solution)/shard_map/slice | solution.py:18
  2.5 0.6 collective-permute-start
  3.0 0.1 collective-permute-start.1
  3.1 2.2 %collective-permute-done = f32[1,16,128,128]{3,2,1,0:T(8,128)S(1)} collective-permute-done((f32[1,16,128,128]{3,2,1,0:T(8,128)S(1)}, f32[1,16,128,128]{3,2,1,0:T(8,128)S(1)}, u32[]{:S(2)}, u32[]{:S(2)}) %collective-permute-start) | collective-permute-done | bytes 1048608 | tf_op jit(solution)/shard_map/ppermute | solution.py:15
  5.3 0.1 constant_dynamic-update-slice_fusion.2
  5.4 0.5 constant_dynamic-update-slice_fusion.1
  5.9 0.9 collective-permute-done.1
  6.8 0.1 constant_dynamic-update-slice_fusion
  7.0 2.9 %collective-permute-start.2 = (f32[6,1,128,128]{3,2,1,0:T(8,128)S(1)}, f32[6,1,128,128]{3,2,1,0:T(8,128)S(1)}, u32[]{:S(2)}, u32[]{:S(2)}) collective-permute-start(f32[6,1,128,128]{3,2,1,0:T(8,128)S(1)} %get-tuple-element.14), channel_id=1, source_target_pairs={{0,2},{2,0},{1,3},{3,1},{4,6},{6,4},{5,7},{7,5},{8,10},{10,8},{9,1... | collective-permute-start | bytes 1179656 | tf_op jit(solution)/shard_map/ppermute | solution.py:15
  9.9 0.1 collective-permute-start.3
  10.0 9.9 %collective-permute-done.2 = f32[6,1,128,128]{3,2,1,0:T(8,128)S(1)} collective-permute-done((f32[6,1,128,128]{3,2,1,0:T(8,128)S(1)}, f32[6,1,128,128]{3,2,1,0:T(8,128)S(1)}, u32[]{:S(2)}, u32[]{:S(2)}) %collective-permute-start.2) | collective-permute-done | bytes 393248 | tf_op jit(solution)/shard_map/ppermute | solution.py:15
  19.9 7.9 %collective-permute-done.3 = f32[6,1,128,128]{3,2,1,0:T(8,128)S(1)} collective-permute-done((f32[6,1,128,128]{3,2,1,0:T(8,128)S(1)}, f32[6,1,128,128]{3,2,1,0:T(8,128)S(1)}, u32[]{:S(2)}, u32[]{:S(2)}) %collective-permute-start.3) | collective-permute-done | bytes 393248 | tf_op jit(solution)/shard_map/ppermute | solution.py:18
  27.8 0.1 pad_maximum_fusion.64
  27.9 1.8 %collective-permute-start.4 = (f32[6,18,1,128]{3,2,1,0:T(1,128)S(1)}, f32[6,18,1,128]{3,2,1,0:T(1,128)S(1)}, u32[]{:S(2)}, u32[]{:S(2)}) collective-permute-start(f32[6,18,1,128]{3,2,1,0:T(1,128)S(1)} %get-tuple-element.8), channel_id=1, source_target_pairs={{0,1},{1,0},{2,3},{3,2},{4,5},{5,4},{6,7},{7,6},{8,9},{9,8},{10,11... | collective-permute-start | bytes 165896 | tf_op jit(solution)/shard_map/ppermute | solution.py:15
  29.7 0.3 collective-permute-start.5
  29.9 2.5 %collective-permute-done.4 = f32[6,18,1,128]{3,2,1,0:T(1,128)S(1)} collective-permute-done((f32[6,18,1,128]{3,2,1,0:T(1,128)S(1)}, f32[6,18,1,128]{3,2,1,0:T(1,128)S(1)}, u32[]{:S(2)}, u32[]{:S(2)}) %collective-permute-start.4) | collective-permute-done | bytes 55328 | tf_op jit(solution)/shard_map/ppermute | solution.py:15
  32.5 1.4 collective-permute-done.5
  33.8 13.8 %fusion.22 = f32[4,16,128,128]{3,2,1,0:T(8,128)S(1)} fusion(f32[4,16,128,128]{3,2,1,0:T(8,128)S(1)} %copy-done, f32[4,16,128,128]{3,2,1,0:T(8,128)} %param.3, f32[4,16,128,128]{3,2,1,0:T(8,128)} %param.4, f32[6,18,1,128]{3,2,1,0:T(1,128)S(1)} %collective-permute-done.5, f32[6,1,128,128]{3,2,1,0:T(8,128)S(1)} %collective-permute-done.3, ...), kind=kLoop, calls=%fused_computation.59 | loop fusion | flops 20971520 | bytes 26062848 | tf_op jit(solution)/shard_map/add | solution.py:40
  47.6 0.1 fusion.31
  47.8 0.5 collective-permute-start.7
  48.3 2.1 %collective-permute-done.6 = f32[1,16,128,128]{3,2,1,0:T(8,128)S(1)} collective-permute-done((f32[1,16,128,128]{3,2,1,0:T(8,128)S(1)}, f32[1,16,128,128]{3,2,1,0:T(8,128)S(1)}, u32[]{:S(2)}, u32[]{:S(2)}) %collective-permute-start.6) | collective-permute-done | bytes 1048608 | tf_op jit(solution)/shard_map/ppermute | solution.py:15
  50.5 1.5 %collective-permute-done.7 = f32[1,16,128,128]{3,2,1,0:T(8,128)S(1)} collective-permute-done((f32[1,16,128,128]{3,2,1,0:T(8,128)S(1)}, f32[1,16,128,128]{3,2,1,0:T(8,128)S(1)}, u32[]{:S(2)}, u32[]{:S(2)}) %collective-permute-start.7) | collective-permute-done | bytes 1048608 | tf_op jit(solution)/shard_map/ppermute | solution.py:18
  52.1 1.6 %collective-permute-start.8 = (f32[6,1,128,128]{3,2,1,0:T(8,128)S(1)}, f32[6,1,128,128]{3,2,1,0:T(8,128)S(1)}, u32[]{:S(2)}, u32[]{:S(2)}) collective-permute-start(f32[6,1,128,128]{3,2,1,0:T(8,128)S(1)} %get-tuple-element.12), channel_id=1, source_target_pairs={{0,2},{2,0},{1,3},{3,1},{4,6},{6,4},{5,7},{7,5},{8,10},{10,8},{9,1... | collective-permute-start | bytes 1179656 | tf_op jit(solution)/shard_map/ppermute | solution.py:15
  53.6 0.5 collective-permute-start.9
  54.2 10.0 %collective-permute-done.8 = f32[6,1,128,128]{3,2,1,0:T(8,128)S(1)} collective-permute-done((f32[6,1,128,128]{3,2,1,0:T(8,128)S(1)}, f32[6,1,128,128]{3,2,1,0:T(8,128)S(1)}, u32[]{:S(2)}, u32[]{:S(2)}) %collective-permute-start.8) | collective-permute-done | bytes 393248 | tf_op jit(solution)/shard_map/ppermute | solution.py:15
  64.1 7.6 %collective-permute-done.9 = f32[6,1,128,128]{3,2,1,0:T(8,128)S(1)} collective-permute-done((f32[6,1,128,128]{3,2,1,0:T(8,128)S(1)}, f32[6,1,128,128]{3,2,1,0:T(8,128)S(1)}, u32[]{:S(2)}, u32[]{:S(2)}) %collective-permute-start.9) | collective-permute-done | bytes 393248 | tf_op jit(solution)/shard_map/ppermute | solution.py:18
  71.8 0.7 collective-permute-start.10
  72.5 1.4 collective-permute-start.11
  73.9 2.1 %collective-permute-done.10 = f32[6,18,1,128]{3,2,1,0:T(1,128)S(1)} collective-permute-done((f32[6,18,1,128]{3,2,1,0:T(1,128)S(1)}, f32[6,18,1,128]{3,2,1,0:T(1,128)S(1)}, u32[]{:S(2)}, u32[]{:S(2)}) %collective-permute-start.10) | collective-permute-done | bytes 55328 | tf_op jit(solution)/shard_map/ppermute | solution.py:15
  76.0 0.6 collective-permute-done.11
  76.6 7.6 %fusion.13 = f32[4,16,128,128]{3,2,1,0:T(8,128)S(1)} fusion(f32[4,16,128,128]{3,2,1,0:T(8,128)S(1)} %copy-done, f32[4,16,128,128]{3,2,1,0:T(8,128)S(1)} %fusion.22, f32[4,16,128,128]{3,2,1,0:T(8,128)S(1)} %copy-done.1, f32[6,18,1,128]{3,2,1,0:T(1,128)S(1)} %collective-permute-done.11, f32[6,1,128,128]{3,2,1,0:T(8,128)S(1)} %collective-permute-done.9, ...), kind=kLoop, calls=%fused_computation.32 | loop fusion | flops 29360128 | bytes 19771392 | tf_op jit(solution)/shard_map/add | solution.py:40
  84.2 0.2 fusion.30
  84.5 0.5 collective-permute-start.13
  85.0 2.1 %collective-permute-done.12 = f32[1,16,128,128]{3,2,1,0:T(8,128)S(1)} collective-permute-done((f32[1,16,128,128]{3,2,1,0:T(8,128)S(1)}, f32[1,16,128,128]{3,2,1,0:T(8,128)S(1)}, u32[]{:S(2)}, u32[]{:S(2)}) %collective-permute-start.12) | collective-permute-done | bytes 1048608 | tf_op jit(solution)/shard_map/ppermute | solution.py:15
  87.2 1.5 %collective-permute-done.13 = f32[1,16,128,128]{3,2,1,0:T(8,128)S(1)} collective-permute-done((f32[1,16,128,128]{3,2,1,0:T(8,128)S(1)}, f32[1,16,128,128]{3,2,1,0:T(8,128)S(1)}, u32[]{:S(2)}, u32[]{:S(2)}) %collective-permute-start.13) | collective-permute-done | bytes 1048608 | tf_op jit(solution)/shard_map/ppermute | solution.py:18
  88.7 1.6 %collective-permute-start.14 = (f32[6,1,128,128]{3,2,1,0:T(8,128)S(1)}, f32[6,1,128,128]{3,2,1,0:T(8,128)S(1)}, u32[]{:S(2)}, u32[]{:S(2)}) collective-permute-start(f32[6,1,128,128]{3,2,1,0:T(8,128)S(1)} %get-tuple-element.10), channel_id=1, source_target_pairs={{0,2},{2,0},{1,3},{3,1},{4,6},{6,4},{5,7},{7,5},{8,10},{10,8},{9,1... | collective-permute-start | bytes 1179656 | tf_op jit(solution)/shard_map/ppermute | solution.py:15
  90.3 0.5 collective-permute-start.15
  90.8 10.0 %collective-permute-done.14 = f32[6,1,128,128]{3,2,1,0:T(8,128)S(1)} collective-permute-done((f32[6,1,128,128]{3,2,1,0:T(8,128)S(1)}, f32[6,1,128,128]{3,2,1,0:T(8,128)S(1)}, u32[]{:S(2)}, u32[]{:S(2)}) %collective-permute-start.14) | collective-permute-done | bytes 393248 | tf_op jit(solution)/shard_map/ppermute | solution.py:15
  100.8 7.6 %collective-permute-done.15 = f32[6,1,128,128]{3,2,1,0:T(8,128)S(1)} collective-permute-done((f32[6,1,128,128]{3,2,1,0:T(8,128)S(1)}, f32[6,1,128,128]{3,2,1,0:T(8,128)S(1)}, u32[]{:S(2)}, u32[]{:S(2)}) %collective-permute-start.15) | collective-permute-done | bytes 393248 | tf_op jit(solution)/shard_map/ppermute | solution.py:18
  108.4 1.5 %collective-permute-start.16 = (f32[6,18,1,128]{3,2,1,0:T(1,128)S(1)}, f32[6,18,1,128]{3,2,1,0:T(1,128)S(1)}, u32[]{:S(2)}, u32[]{:S(2)}) collective-permute-start(f32[6,18,1,128]{3,2,1,0:T(1,128)S(1)} %get-tuple-element.4), channel_id=1, source_target_pairs={{0,1},{1,0},{2,3},{3,2},{4,5},{5,4},{6,7},{7,6},{8,9},{9,8},{10,11... | collective-permute-start | bytes 165896 | tf_op jit(solution)/shard_map/ppermute | solution.py:15
  109.9 0.6 collective-permute-start.17
  110.5 2.2 %collective-permute-done.16 = f32[6,18,1,128]{3,2,1,0:T(1,128)S(1)} collective-permute-done((f32[6,18,1,128]{3,2,1,0:T(1,128)S(1)}, f32[6,18,1,128]{3,2,1,0:T(1,128)S(1)}, u32[]{:S(2)}, u32[]{:S(2)}) %collective-permute-start.16) | collective-permute-done | bytes 55328 | tf_op jit(solution)/shard_map/ppermute | solution.py:15
  112.7 1.4 collective-permute-done.17
  114.1 9.3 %fusion.27 = (f32[4,16,128]{2,1,0:T(8,128)S(1)}, f32[4,16,128,128]{3,2,1,0:T(8,128)}) fusion(f32[4,16,128,128]{3,2,1,0:T(8,128)S(1)} %copy-done, f32[4,16,128,128]{3,2,1,0:T(8,128)S(1)} %fusion.13, f32[4,16,128,128]{3,2,1,0:T(8,128)S(1)} %copy-done.1, f32[6,18,1,128]{3,2,1,0:T(1,128)S(1)} %collective-permute-done.17, ...), kind=kLoop, calls=%fused_computation.99 | loop fusion | flops 30400512 | bytes 19804160 | tf_op jit(solution)/shard_map/reduce_sum | solution.py:48
  123.4 7.4 %psum.7 = f32[4,16,1,128]{3,1,0,2:T(8,128)S(1)} all-reduce(f32[4,16,1,128]{3,1,0,2:T(8,128)S(1)} %bitcast.5), channel_id=1, replica_groups=mesh['trial'=4,'south'=2,'east'=2,'down'=2] {'down'}, use_global_device_ids=true, to_apply=%region_1.0 | all-reduce | flops 8192 | bytes 65536 | tf_op jit(solution)/shard_map/psum | solution.py:48
  130.8 3.0 %multiply_reduce_fusion = f32[4,16,128]{2,1,0:T(8,128)S(1)} fusion(f32[4,16,128,128]{3,2,1,0:T(8,128)} %get-tuple-element.3, f32[4,16,128]{2,1,0:T(8,128)S(1)} %multiply_bitcast_fusion), kind=kLoop, calls=%fused_computation.73 | loop fusion | flops 3137536 | bytes 4259840 | tf_op jit(solution)/shard_map/reduce_sum | solution.py:51
  133.8 4.6 %all-gather = f32[8,16,128]{2,1,0:T(8,128)S(1)} all-gather(f32[4,16,128]{2,1,0:T(8,128)S(1)} %multiply_reduce_fusion), channel_id=2, replica_groups=mesh['trial'=4,'south'=2,'east'=2,'down'=2] {'down'}, dimensions={0}, use_global_device_ids=true | all-gather | bytes 98304 | tf_op jit(solution)/shard_map/all_gather | solution.py:51
  138.4 5.2 %subtract_multiply_fusion = f32[4,16,128,128]{3,2,1,0:T(8,128)} fusion(f32[4,16,128,128]{3,2,1,0:T(8,128)} %get-tuple-element.3, f32[4,16,128]{2,1,0:T(8,128)S(1)} %add_rsqrt_fusion, f32[4,16,128]{2,1,0:T(8,128)S(1)} %multiply_bitcast_fusion), kind=kLoop, calls=%fused_computation.74 | loop fusion | flops 2097152 | bytes 8454144 | tf_op jit(solution)/shard_map/mul | solution.py:54
  (18 shorter events, 0.5 us)
Async XLA Ops:
  0.6 4.8 %copy-start.3 = (f32[4,16,128,128]{3,2,1,0:T(8,128)S(1)}, f32[4,16,128,128]{3,2,1,0:T(8,128)}, u32[]{:S(2)}) copy-start(f32[4,16,128,128]{3,2,1,0:T(8,128)} %param.3) | copy-start | bytes 12582916
  2.5 2.8 %collective-permute-start = (f32[1,16,128,128]{3,2,1,0:T(8,128)S(1)}, f32[1,16,128,128]{3,2,1,0:T(8,128)S(1)}, u32[]{:S(2)}, u32[]{:S(2)}) collective-permute-start(f32[1,16,128,128]{3,2,1,0:T(8,128)S(1)} %get-tuple-element.21), channel_id=1, source_target_pairs={{0,4},{4,0},{1,5},{5,1},{2,6},{6,2},{3,7},{7,3},{8,12},{12,8},{9,1... | collective-permute-start | bytes 3145736 | tf_op jit(solution)/shard_map/ppermute | solution.py:15
  3.0 3.8 %collective-permute-start.1 = (f32[1,16,128,128]{3,2,1,0:T(8,128)S(1)}, f32[1,16,128,128]{3,2,1,0:T(8,128)S(1)}, u32[]{:S(2)}, u32[]{:S(2)}) collective-permute-start(f32[1,16,128,128]{3,2,1,0:T(8,128)S(1)} %get-tuple-element.20), channel_id=1, source_target_pairs={{4,0},{0,4},{5,1},{1,5},{6,2},{2,6},{7,3},{3,7},{12,8},{8,12},{13,... | collective-permute-start | bytes 3145736 | tf_op jit(solution)/shard_map/ppermute | solution.py:18
  6.9 25.5 %copy-start.2 = (f32[6,16,128,128]{3,2,1,0:T(8,128)}, f32[6,16,128,128]{3,2,1,0:T(8,128)S(1)}, u32[]{:S(2)}) copy-start(f32[6,16,128,128]{3,2,1,0:T(8,128)S(1)} %constant_dynamic-update-slice_fusion) | copy-start | bytes 18874372
  6.9 26.9 %copy-start = (f32[4,16,128,128]{3,2,1,0:T(8,128)S(1)}, f32[4,16,128,128]{3,2,1,0:T(8,128)}, u32[]{:S(2)}) copy-start(f32[4,16,128,128]{3,2,1,0:T(8,128)} %param.5) | copy-start | bytes 12582916
  7.0 12.9 %collective-permute-start.2 = (f32[6,1,128,128]{3,2,1,0:T(8,128)S(1)}, f32[6,1,128,128]{3,2,1,0:T(8,128)S(1)}, u32[]{:S(2)}, u32[]{:S(2)}) collective-permute-start(f32[6,1,128,128]{3,2,1,0:T(8,128)S(1)} %get-tuple-element.14), channel_id=1, source_target_pairs={{0,2},{2,0},{1,3},{3,1},{4,6},{6,4},{5,7},{7,5},{8,10},{10,8},{9,1... | collective-permute-start | bytes 1179656 | tf_op jit(solution)/shard_map/ppermute | solution.py:15
  9.9 17.8 %collective-permute-start.3 = (f32[6,1,128,128]{3,2,1,0:T(8,128)S(1)}, f32[6,1,128,128]{3,2,1,0:T(8,128)S(1)}, u32[]{:S(2)}, u32[]{:S(2)}) collective-permute-start(f32[6,1,128,128]{3,2,1,0:T(8,128)S(1)} %get-tuple-element.15), channel_id=1, source_target_pairs={{2,0},{0,2},{3,1},{1,3},{6,4},{4,6},{7,5},{5,7},{10,8},{8,10},{11,... | collective-permute-start | bytes 1179656 | tf_op jit(solution)/shard_map/ppermute | solution.py:18
  27.9 4.6 %collective-permute-start.4 = (f32[6,18,1,128]{3,2,1,0:T(1,128)S(1)}, f32[6,18,1,128]{3,2,1,0:T(1,128)S(1)}, u32[]{:S(2)}, u32[]{:S(2)}) collective-permute-start(f32[6,18,1,128]{3,2,1,0:T(1,128)S(1)} %get-tuple-element.8), channel_id=1, source_target_pairs={{0,1},{1,0},{2,3},{3,2},{4,5},{5,4},{6,7},{7,6},{8,9},{9,8},{10,11... | collective-permute-start | bytes 165896 | tf_op jit(solution)/shard_map/ppermute | solution.py:15
  29.7 4.2 %collective-permute-start.5 = (f32[6,18,1,128]{3,2,1,0:T(1,128)S(1)}, f32[6,18,1,128]{3,2,1,0:T(1,128)S(1)}, u32[]{:S(2)}, u32[]{:S(2)}) collective-permute-start(f32[6,18,1,128]{3,2,1,0:T(1,128)S(1)} %get-tuple-element.9), channel_id=1, source_target_pairs={{1,0},{0,1},{3,2},{2,3},{5,4},{4,5},{7,6},{6,7},{9,8},{8,9},{11,10... | collective-permute-start | bytes 165896 | tf_op jit(solution)/shard_map/ppermute | solution.py:18
  47.8 2.7 %collective-permute-start.6 = (f32[1,16,128,128]{3,2,1,0:T(8,128)S(1)}, f32[1,16,128,128]{3,2,1,0:T(8,128)S(1)}, u32[]{:S(2)}, u32[]{:S(2)}) collective-permute-start(f32[1,16,128,128]{3,2,1,0:T(8,128)S(1)} %get-tuple-element.18), channel_id=1, source_target_pairs={{0,4},{4,0},{1,5},{5,1},{2,6},{6,2},{3,7},{7,3},{8,12},{12,8},{9,1... | collective-permute-start | bytes 3145736 | tf_op jit(solution)/shard_map/ppermute | solution.py:15
  47.8 4.1 %collective-permute-start.7 = (f32[1,16,128,128]{3,2,1,0:T(8,128)S(1)}, f32[1,16,128,128]{3,2,1,0:T(8,128)S(1)}, u32[]{:S(2)}, u32[]{:S(2)}) collective-permute-start(f32[1,16,128,128]{3,2,1,0:T(8,128)S(1)} %get-tuple-element.19), channel_id=1, source_target_pairs={{4,0},{0,4},{5,1},{1,5},{6,2},{2,6},{7,3},{3,7},{12,8},{8,12},{13,... | collective-permute-start | bytes 3145736 | tf_op jit(solution)/shard_map/ppermute | solution.py:18
  52.1 24.6 %copy-start.1 = (f32[4,16,128,128]{3,2,1,0:T(8,128)S(1)}, f32[4,16,128,128]{3,2,1,0:T(8,128)}, u32[]{:S(2)}) copy-start(f32[4,16,128,128]{3,2,1,0:T(8,128)} %param.4) | copy-start | bytes 12582916
  52.1 12.1 %collective-permute-start.8 = (f32[6,1,128,128]{3,2,1,0:T(8,128)S(1)}, f32[6,1,128,128]{3,2,1,0:T(8,128)S(1)}, u32[]{:S(2)}, u32[]{:S(2)}) collective-permute-start(f32[6,1,128,128]{3,2,1,0:T(8,128)S(1)} %get-tuple-element.12), channel_id=1, source_target_pairs={{0,2},{2,0},{1,3},{3,1},{4,6},{6,4},{5,7},{7,5},{8,10},{10,8},{9,1... | collective-permute-start | bytes 1179656 | tf_op jit(solution)/shard_map/ppermute | solution.py:15
  53.6 18.1 %collective-permute-start.9 = (f32[6,1,128,128]{3,2,1,0:T(8,128)S(1)}, f32[6,1,128,128]{3,2,1,0:T(8,128)S(1)}, u32[]{:S(2)}, u32[]{:S(2)}) collective-permute-start(f32[6,1,128,128]{3,2,1,0:T(8,128)S(1)} %get-tuple-element.13), channel_id=1, source_target_pairs={{2,0},{0,2},{3,1},{1,3},{6,4},{4,6},{7,5},{5,7},{10,8},{8,10},{11,... | collective-permute-start | bytes 1179656 | tf_op jit(solution)/shard_map/ppermute | solution.py:18
  71.8 4.2 %collective-permute-start.10 = (f32[6,18,1,128]{3,2,1,0:T(1,128)S(1)}, f32[6,18,1,128]{3,2,1,0:T(1,128)S(1)}, u32[]{:S(2)}, u32[]{:S(2)}) collective-permute-start(f32[6,18,1,128]{3,2,1,0:T(1,128)S(1)} %get-tuple-element.6), channel_id=1, source_target_pairs={{0,1},{1,0},{2,3},{3,2},{4,5},{5,4},{6,7},{7,6},{8,9},{9,8},{10,11... | collective-permute-start | bytes 165896 | tf_op jit(solution)/shard_map/ppermute | solution.py:15
  72.5 4.2 %collective-permute-start.11 = (f32[6,18,1,128]{3,2,1,0:T(1,128)S(1)}, f32[6,18,1,128]{3,2,1,0:T(1,128)S(1)}, u32[]{:S(2)}, u32[]{:S(2)}) collective-permute-start(f32[6,18,1,128]{3,2,1,0:T(1,128)S(1)} %get-tuple-element.7), channel_id=1, source_target_pairs={{1,0},{0,1},{3,2},{2,3},{5,4},{4,5},{7,6},{6,7},{9,8},{8,9},{11,10... | collective-permute-start | bytes 165896 | tf_op jit(solution)/shard_map/ppermute | solution.py:18
  84.4 2.7 %collective-permute-start.12 = (f32[1,16,128,128]{3,2,1,0:T(8,128)S(1)}, f32[1,16,128,128]{3,2,1,0:T(8,128)S(1)}, u32[]{:S(2)}, u32[]{:S(2)}) collective-permute-start(f32[1,16,128,128]{3,2,1,0:T(8,128)S(1)} %get-tuple-element.16), channel_id=1, source_target_pairs={{0,4},{4,0},{1,5},{5,1},{2,6},{6,2},{3,7},{7,3},{8,12},{12,8},{9,1... | collective-permute-start | bytes 3145736 | tf_op jit(solution)/shard_map/ppermute | solution.py:15
  84.5 4.1 %collective-permute-start.13 = (f32[1,16,128,128]{3,2,1,0:T(8,128)S(1)}, f32[1,16,128,128]{3,2,1,0:T(8,128)S(1)}, u32[]{:S(2)}, u32[]{:S(2)}) collective-permute-start(f32[1,16,128,128]{3,2,1,0:T(8,128)S(1)} %get-tuple-element.17), channel_id=1, source_target_pairs={{4,0},{0,4},{5,1},{1,5},{6,2},{2,6},{7,3},{3,7},{12,8},{8,12},{13,... | collective-permute-start | bytes 3145736 | tf_op jit(solution)/shard_map/ppermute | solution.py:18
  88.7 12.1 %collective-permute-start.14 = (f32[6,1,128,128]{3,2,1,0:T(8,128)S(1)}, f32[6,1,128,128]{3,2,1,0:T(8,128)S(1)}, u32[]{:S(2)}, u32[]{:S(2)}) collective-permute-start(f32[6,1,128,128]{3,2,1,0:T(8,128)S(1)} %get-tuple-element.10), channel_id=1, source_target_pairs={{0,2},{2,0},{1,3},{3,1},{4,6},{6,4},{5,7},{7,5},{8,10},{10,8},{9,1... | collective-permute-start | bytes 1179656 | tf_op jit(solution)/shard_map/ppermute | solution.py:15
  90.3 18.1 %collective-permute-start.15 = (f32[6,1,128,128]{3,2,1,0:T(8,128)S(1)}, f32[6,1,128,128]{3,2,1,0:T(8,128)S(1)}, u32[]{:S(2)}, u32[]{:S(2)}) collective-permute-start(f32[6,1,128,128]{3,2,1,0:T(8,128)S(1)} %get-tuple-element.11), channel_id=1, source_target_pairs={{2,0},{0,2},{3,1},{1,3},{6,4},{4,6},{7,5},{5,7},{10,8},{8,10},{11,... | collective-permute-start | bytes 1179656 | tf_op jit(solution)/shard_map/ppermute | solution.py:18
  108.4 4.3 %collective-permute-start.16 = (f32[6,18,1,128]{3,2,1,0:T(1,128)S(1)}, f32[6,18,1,128]{3,2,1,0:T(1,128)S(1)}, u32[]{:S(2)}, u32[]{:S(2)}) collective-permute-start(f32[6,18,1,128]{3,2,1,0:T(1,128)S(1)} %get-tuple-element.4), channel_id=1, source_target_pairs={{0,1},{1,0},{2,3},{3,2},{4,5},{5,4},{6,7},{7,6},{8,9},{9,8},{10,11... | collective-permute-start | bytes 165896 | tf_op jit(solution)/shard_map/ppermute | solution.py:15
  109.9 4.2 %collective-permute-start.17 = (f32[6,18,1,128]{3,2,1,0:T(1,128)S(1)}, f32[6,18,1,128]{3,2,1,0:T(1,128)S(1)}, u32[]{:S(2)}, u32[]{:S(2)}) collective-permute-start(f32[6,18,1,128]{3,2,1,0:T(1,128)S(1)} %get-tuple-element.5), channel_id=1, source_target_pairs={{1,0},{0,1},{3,2},{2,3},{5,4},{4,5},{7,6},{6,7},{9,8},{8,9},{11,10... | collective-permute-start | bytes 165896 | tf_op jit(solution)/shard_map/ppermute | solution.py:18
